TPU v7x, 32 devices: a whole 2x2x4 slice. The times are simulated.
32 devices in a mesh: groups: 2 (over y), fsdp: 4 (over z), mp: 2 (over x), sub: 2 (over core).
Axes of the slice: x: 2, y: 2, z: 4, core: 2. Of those that a mesh axis runs over, the one named last changes fastest.
Arguments:
- hidden: bfloat16 [128, 36864], P(('groups', 'fsdp', 'sub'), 'mp'), parts along dimension 0, may hold values from -6 to 6
- residual: bfloat16 [128, 4608], P(('groups', 'fsdp', 'sub')), parts along dimension 0, may hold values from -6 to 6
- down_packed: int32 [4608, 4608], P('mp', 'fsdp'), may hold values from -2147483648 to 2147483646
- down_scale: bfloat16 [288, 4608], P('mp', 'fsdp'), may hold values from 0.00049972534 to 0.0019989014
- post_gain: float32 [4608], replicated, may hold values from 0.1 to 1.9
- final_gain: float32 [4608], replicated, may hold values from 0.1 to 1.9
- embed_packed: int32 [8192, 576], P(('fsdp', 'mp', 'sub')), may hold values from -2147483648 to 2147483646
- embed_scale: bfloat16 [8192, 36], P(('fsdp', 'mp', 'sub')), may hold values from 0.0059814453 to 0.029907227
- targets: int32 [128], P(('groups', 'fsdp', 'sub')), parts along dimension 0, may hold values from 0 to 8191
- loss_mask: int32 [128], P(('groups', 'fsdp', 'sub')), parts along dimension 0, may hold values 0 or 1
Outputs:
- token_loss: float32 [128], P(('groups', 'fsdp', 'sub')), parts along dimension 0
- mean_loss: float32 [2], P('groups'), parts along dimension 0
There are 2 independent parts, one for each index of `groups`. A program takes and returns all parts, laid end to end along the dimension named above; an argument that names none is the same for every part. Nothing has to cross between parts.
Inputs may be any that keep to these rules, and one draw needn't show every extreme that they name: `down_packed`: bits 4 k to 4 k + 3 of the word in row r hold the signed code of row 8 r + k of the down projection, k = 0..7. `embed_packed`: bits 4 k to 4 k + 3 of the word in column j hold the signed code of column k * 576 + j of the embedding, k = 0..7.
All inputs are finite; a program needn't handle non-finite values. No bound on the sum of `loss_mask` on one device may be relied on, other than what follows from the above.
Results may differ from a plain program's by a relative error of at most 0.00097.
Values may be sent and summed in bfloat16 or wider, within the bound.
A program may use at most 128 MiB of HBM per device.

v0:
```python
import jax
import jax.numpy as jnp
from jax import lax
from jax.sharding import PartitionSpec as P

EPS = 1e-06
CAP = 30.0


def signed_planes(words):
    shifts = (28 - 4 * jnp.arange(8, dtype=jnp.int32))[None, :, None]
    lifted = jnp.left_shift(words[:, None, :], shifts)
    return jnp.right_shift(lifted, 28)


def dequant_down(words, scales):
    cols = words.shape[1]
    codes = signed_planes(words).astype(jnp.bfloat16)
    grouped = codes.reshape(scales.shape[0], -1, cols) * scales[:, None, :]
    return grouped.reshape(-1, cols)


def dequant_embed(words, scales):
    rows = words.shape[0]
    codes = signed_planes(words).astype(jnp.bfloat16)
    grouped = codes.reshape(rows, scales.shape[1], -1) * scales[:, :, None]
    return grouped.reshape(rows, -1)


def normalize_rows(ffn, residual, post_gain, final_gain):
    ffn = lax.psum(ffn, "mp")
    normed = ffn * lax.rsqrt(jnp.mean(ffn * ffn, axis=-1, keepdims=True) + EPS) * post_gain
    stream = residual.astype(jnp.float32) + normed
    return (
        stream * lax.rsqrt(jnp.mean(stream * stream, axis=-1, keepdims=True) + EPS) * final_gain
    ).astype(jnp.bfloat16)


def on_device(
    hidden,
    residual,
    down_packed,
    down_scale,
    post_gain,
    final_gain,
    embed_packed,
    embed_scale,
    targets,
    loss_mask,
):
    tok_rows = hidden.shape[0]
    local_weight = dequant_down(down_packed, down_scale)
    partial_cols = jnp.dot(
        lax.all_gather(hidden, "fsdp", axis=0, tiled=True),
        local_weight,
        preferred_element_type=jnp.float32,
    )
    ffn = lax.all_to_all(partial_cols, "fsdp", split_axis=0, concat_axis=1, tiled=True)
    states = normalize_rows(ffn, residual, post_gain, final_gain)
    all_states, all_targets = (
        lax.all_gather(states, ("fsdp", "sub"), axis=0, tiled=True),
        lax.all_gather(targets, ("fsdp", "sub"), axis=0, tiled=True),
    )
    embed = dequant_embed(embed_packed, embed_scale)
    logits = lax.dot_general(
        all_states, embed, (((1,), (1,)), ((), ())), preferred_element_type=jnp.float32
    )
    capped = CAP * jnp.tanh(logits / CAP)
    vocab_rows = embed.shape[0]
    first_id = lax.axis_index(("fsdp", "mp", "sub")) * vocab_rows
    ids = first_id + jnp.arange(vocab_rows, dtype=jnp.int32)
    hits = all_targets[:, None] == ids[None, :]
    exp_sums, target_logits = lax.psum(
        (jnp.sum(jnp.exp(capped), axis=1), jnp.sum(jnp.where(hits, capped, 0.0), axis=1)),
        ("fsdp", "mp", "sub"),
    )
    own_start = lax.axis_index(("fsdp", "sub")) * tok_rows
    own_sums = lax.dynamic_slice_in_dim(exp_sums, own_start, tok_rows, 0)
    own_targets = lax.dynamic_slice_in_dim(target_logits, own_start, tok_rows, 0)
    weights = loss_mask.astype(jnp.float32)
    token_loss = weights * (jnp.log(own_sums) - own_targets)
    loss_sum, count = lax.psum((jnp.sum(token_loss), jnp.sum(weights)), ("fsdp", "sub"))
    mean_loss = (loss_sum / jnp.maximum(count, 1.0)).reshape(1)
    return (token_loss, mean_loss)


def solution(mesh):
    return jax.shard_map(
        on_device,
        mesh=mesh,
        in_specs=(
            P(("groups", "fsdp", "sub"), "mp"),
            P(("groups", "fsdp", "sub"), None),
            P("mp", "fsdp"),
            P("mp", "fsdp"),
            P(),
            P(),
            P(("fsdp", "mp", "sub"), None),
            P(("fsdp", "mp", "sub"), None),
            P(("groups", "fsdp", "sub")),
            P(("groups", "fsdp", "sub")),
        ),
        out_specs=(P(("groups", "fsdp", "sub")), P("groups")),
        check_vma=False,
    )
```

profile of v0, /device:TPU:0, one launch (start us, length us, event | category | flops | bytes accessed | tf_op | source)
XLA Modules:
  0.0 167.8 jit_solution(12297695420085963303)
XLA Ops:
  7.2 0.0 all-gather.2.cloned.1.call-start
  7.2 0.7 all-gather.2.cloned.1.call-update
  7.9 0.0 all-reduce.5.cloned.1.call-start
  8.0 0.1 shift_left.49
  8.1 17.8 %fusion.2 = bf16[18432,1152]{1,0:T(8,128)(2,1)} fusion(s32[18432]{0:T(1024)S(1)} %broadcast_bitcast_fusion, s32[2304,1152]{1,0:T(8,128)} %param.12, bf16[144,1152]{1,0:T(8,128)(2,1)} %param.13), kind=kLoop, calls=%fused_computation.3 | loop fusion | flops 148635648 | bytes 53489664 | tf_op jit(solution)/shard_map/mul | solution.py:19
  26.0 16.6 %all-gather.2.cloned.1.call-done = bf16[32,18432]{1,0:T(8,128)(2,1)} async-done(((bf16[8,18432]{1,0:T(8,128)(2,1)}), bf16[32,18432]{1,0:T(8,128)(2,1)}) %all-gather.2.cloned.1.call-update) | async-done | bytes 1179664 | tf_op jit(solution)/shard_map/all_gather | solution.py:54
  42.6 15.8 %convolution_bitcast_fusion = f32[4,8,1152]{2,1,0:T(8,128)S(1)} fusion(bf16[32,18432]{1,0:T(8,128)(2,1)} %all-gather.2.cloned.1.call-done, bf16[18432,1152]{1,0:T(8,128)(2,1)} %fusion.2), kind=kOutput, calls=%fused_computation.8 | convolution fusion | flops 1358954496 | bytes 43794432 | tf_op jit(solution)/shard_map/dot_general | solution.py:53
  58.4 9.7 %all_to_all.19 = f32[4,8,1152]{2,1,0:T(8,128)} all-to-all(f32[4,8,1152]{2,1,0:T(8,128)S(1)} %convolution_bitcast_fusion), channel_id=1, replica_groups=mesh['groups'=2,'fsdp'=4,'mp'=2,'sub'=2] {'fsdp'}, dimensions={0} | all-to-all | bytes 294912 | tf_op jit(solution)/shard_map/all_to_all | solution.py:58
  68.1 0.0 all-reduce.5.cloned.1.call-update
  68.1 0.1 shift_left.56
  68.2 0.1 shift_left.57
  68.3 0.6 dynamic-slice
  69.5 0.2 dynamic-update-slice
  69.8 3.6 %fusion.5 = bf16[512,4608]{0,1:T(8,128)(2,1)} fusion(s32[4608]{0:T(1024)S(1)} %shift_left.57, s32[512,576]{0,1:T(8,128)S(1)} %copy-done, bf16[512,36]{0,1:T(8,128)(2,1)S(1)} %copy-done.3), kind=kLoop, calls=%fused_computation.7 | loop fusion | flops 16515072 | bytes 5953536 | tf_op jit(solution)/shard_map/mul | solution.py:26
  73.4 6.5 %all-reduce = s32[64]{0:T(128)S(1)} all-reduce(s32[64]{0:T(128)S(1)} %dynamic-update-slice), channel_id=1, replica_groups=mesh['groups'=2,'fsdp'=4,'mp'=2,'sub'=2] {'fsdp','sub'}, use_global_device_ids=true, to_apply=%add | all-reduce | flops 64 | bytes 512
  79.8 8.8 %all-reduce.5.cloned.1.call-done = f32[8,4608]{1,0:T(8,128)} async-done(((f32[8,4608]{1,0:T(8,128)}), f32[8,4608]{1,0:T(8,128)}) %all-reduce.5.cloned.1.call-update) | async-done | bytes 147472 | tf_op jit(solution)/shard_map/psum | solution.py:31
  88.7 1.1 multiply_reduce_fusion.1
  89.8 1.1 multiply_reduce_fusion
  90.9 1.0 multiply_convert_fusion
  91.9 15.1 %all_gather.10 = bf16[64,4608]{1,0:T(8,128)(2,1)S(1)} all-gather(bf16[8,4608]{1,0:T(8,128)(2,1)S(1)} %multiply_convert_fusion), channel_id=1, replica_groups=mesh['groups'=2,'fsdp'=4,'mp'=2,'sub'=2] {'fsdp','sub'}, dimensions={0}, use_global_device_ids=true | all-gather | bytes 663552 | tf_op jit(solution)/shard_map/all_gather | solution.py:61
  107.0 3.4 %exponential_reduce_fusion = (f32[64]{0:T(128)S(1)}, f32[64]{0:T(128)S(1)}) fusion(s32[512]{0:T(512)S(1)} %iota_add_fusion, s32[64]{0:T(128)S(1)} %all-reduce, bf16[64,4608]{1,0:T(8,128)(2,1)S(1)} %all_gather.10, bf16[512,4608]{0,1:T(8,128)(2,1)} %fusion.5), kind=kOutput, calls=%fused_computation.17 | convolution fusion | flops 302186368 | bytes 5311232 | tf_op jit(solution)/shard_map/dot_general | solution.py:65
  110.4 32.7 %all-reduce.1 = (f32[64]{0:T(128)S(1)}, f32[64]{0:T(128)S(1)}) all-reduce(f32[64]{0:T(128)S(1)} %get-tuple-element.3, f32[64]{0:T(128)S(1)} %get-tuple-element.2), channel_id=1, replica_groups=mesh['groups'=2,'fsdp'=4,'mp'=2,'sub'=2] {'fsdp','mp','sub'}, use_global_device_ids=true, to_apply=%region_6.7 | all-reduce | flops 128 | bytes 1024 | tf_op jit(solution)/shard_map/psum | solution.py:73
  143.1 1.3 fusion.8
  144.4 14.2 %all-reduce.2 = (f32[]{:T(128)}, f32[]{:T(128)}) all-reduce(f32[]{:T(128)} %get-tuple-element.8, f32[]{:T(128)} %get-tuple-element.10), channel_id=1, replica_groups=mesh['groups'=2,'fsdp'=4,'mp'=2,'sub'=2] {'fsdp','sub'}, use_global_device_ids=true, to_apply=%region_8.9 | all-reduce | flops 2 | bytes 16 | tf_op jit(solution)/shard_map/psum | solution.py:82
  (23 shorter events, 0.1 us)
Async XLA Ops:
  7.2 35.4 %all-gather.2.cloned.1.call-start = ((), (), s32[]{:S(2)}) async-start(), calls=%async_computation.1 | async-start | bytes 1474560 | tf_op jit(solution)/shard_map/all_gather | solution.py:54
  7.9 80.8 %all-reduce.5.cloned.1.call-start = ((), (), s32[]{:S(2)}) async-start(), calls=%async_computation.2 | async-start | bytes 294912 | tf_op jit(solution)/shard_map/psum | solution.py:31
  25.9 42.4 %copy-start.7 = (u32[32]{0:T(128)S(1)}, u32[32]{0:T(128)}, u32[]{:S(2)}) copy-start(u32[32]{0:T(128)} %constant.48) | copy-start | bytes 388
  25.9 43.6 %copy-start.6 = (s32[8]{0:T(128)S(1)}, s32[8]{0:T(128)}, u32[]{:S(2)}) copy-start(s32[8]{0:T(128)} %param.18) | copy-start | bytes 100
  25.9 43.9 %copy-start = (s32[512,576]{0,1:T(8,128)S(1)}, s32[512,576]{0,1:T(8,128)}, u32[]{:S(2)}) copy-start(s32[512,576]{0,1:T(8,128)} %param.16) | copy-start | bytes 3538948
  25.9 43.8 %copy-start.3 = (bf16[512,36]{0,1:T(8,128)(2,1)S(1)}, bf16[512,36]{0,1:T(8,128)(2,1)}, u32[]{:S(2)}) copy-start(bf16[512,36]{0,1:T(8,128)(2,1)} %param.17) | copy-start | bytes 110596
  26.0 63.8 %copy-start.1 = (bf16[8,4608]{1,0:T(8,128)(2,1)S(1)}, bf16[8,4608]{1,0:T(8,128)(2,1)}, u32[]{:S(2)}) copy-start(bf16[8,4608]{1,0:T(8,128)(2,1)} %param.11) | copy-start | bytes 221188
  26.0 63.8 %copy-start.2 = (f32[4608]{0:T(1024)S(1)}, f32[4608]{0:T(1024)}, u32[]{:S(2)}) copy-start(f32[4608]{0:T(1024)} %param.14) | copy-start | bytes 55300
  26.0 64.9 %copy-start.4 = (f32[4608]{0:T(1024)S(1)}, f32[4608]{0:T(1024)}, u32[]{:S(2)}) copy-start(f32[4608]{0:T(1024)} %param.15) | copy-start | bytes 55300
  58.4 84.8 %copy-start.5 = (s32[8]{0:T(128)S(1)}, s32[8]{0:T(128)}, u32[]{:S(2)}) copy-start(s32[8]{0:T(128)} %param.19) | copy-start | bytes 100
Sparse Core Ops, SparseCore 0:
  9.5 32.9 all-gather.1
  68.2 20.3 all-reduce.4
where the time goes:
time: 168 us
  blocking collectives  78.2 us (47%)
  waiting for transfers between devices  26.1 us (16%)
  other arithmetic  25.9 us (15%)
  matrix products  19.2 us (11%)
  between operations  17.2 us (10%)
    psum x1, blocking collectives, on_device(): lax.psum((jnp.sum(jnp.exp(capped), axis=1), jnp.sum(jnp.where(hits, cappe...  32.7 us
    mul x1, other arithmetic, dequant_down(): grouped = codes.reshape(scales.shape[0], -1, cols) * scales[:, None, :]  17.8 us
    all_gather x1, waiting for transfers between devices, on_device(): lax.all_gather(hidden, 'fsdp', axis=0, tiled=True)  16.6 us
    dot_general x1, matrix products, on_device(): jnp.dot(lax.all_gather(hidden, 'fsdp', axis=0, tiled=True), local_weight,...  15.8 us
    all_gather x1, blocking collectives, on_device(): lax.all_gather(states, ('fsdp', 'sub'), axis=0, tiled=True)  15.1 us
    psum x1, blocking collectives, on_device(): lax.psum((jnp.sum(token_loss), jnp.sum(weights)), ('fsdp', 'sub'))  14.2 us
    all_to_all x1, blocking collectives, on_device(): lax.all_to_all(partial_cols, 'fsdp', split_axis=0, concat_axis=1, tiled=T...  9.71 us
    psum x1, waiting for transfers between devices, normalize_rows(): ffn = lax.psum(ffn, 'mp')  8.84 us
  transfers between devices with their start and end apart: 2, of which 2 were waited for; matrix products, arithmetic and copies ran while one was open for 13% of the time, Pallas kernels for 0%

commit v1 on v0

--- a/solution.py
+++ b/solution.py
@@ -5,6 +5,11 @@
 
 EPS = 1e-06
 CAP = 30.0
+
+
+def swapped_in(block, name, dim):
+    sent = jnp.stack([block] * lax.axis_size(name))
+    return jnp.concatenate(lax.all_to_all(sent, name, 0, 0), axis=dim)
 
 
 def signed_planes(words):
@@ -58,7 +63,7 @@
     ffn = lax.all_to_all(partial_cols, "fsdp", split_axis=0, concat_axis=1, tiled=True)
     states = normalize_rows(ffn, residual, post_gain, final_gain)
     all_states, all_targets = (
-        lax.all_gather(states, ("fsdp", "sub"), axis=0, tiled=True),
+        swapped_in(states, ("fsdp", "sub"), 0),
         lax.all_gather(targets, ("fsdp", "sub"), axis=0, tiled=True),
     )
     embed = dequant_embed(embed_packed, embed_scale)

time: 168 us -> 178 us (1.060)
  waiting for transfers between devices: 26.1 us -> 37.8 us
  blocking collectives: 78.2 us -> 69.6 us
  starting transfers between devices: 0.08 us -> 4.68 us
  local copies, waits for them, and re-layouts: 1.12 us -> 3.18 us
    all_gather x1 -> x0, blocking collectives: 15.1 us -> none  [on_device(): lax.all_gather(states, ('fsdp', 'sub'), axis=0, tiled=True)]
    psum x1, waiting for transfers between devices: 8.84 us -> 20.6 us  [normalize_rows(): ffn = lax.psum(ffn, 'mp')]
    unnamed x1, blocking collectives: 6.46 us -> 15.3 us
    all_to_all x0 -> x1, starting transfers between devices: none -> 4.61 us  [swapped_in(): return jnp.concatenate(lax.all_to_all(sent, name, 0, 0), axis=dim)]
    psum x1, blocking collectives: 32.7 us -> 30.4 us  [on_device(): lax.psum((jnp.sum(jnp.exp(capped), axis=1), jnp.sum(jnp.where(hits, cappe...]
  transfers between devices with their start and end apart: 2 -> 3, of which waited for: 2 -> 2; matrix products, arithmetic and copies ran while one was open for 13% -> 13% of each run, Pallas kernels for 0% -> 0%
where the time goes in v1:
time: 178 us
  blocking collectives  69.6 us (39%)
  waiting for transfers between devices  37.8 us (21%)
  other arithmetic  25.9 us (15%)
  matrix products  19.2 us (11%)
  between operations  17.2 us (10%)
  starting transfers between devices  4.68 us (3%)
  local copies, waits for them, and re-layouts  3.18 us (2%)
    psum x1, blocking collectives, on_device(): lax.psum((jnp.sum(jnp.exp(capped), axis=1), jnp.sum(jnp.where(hits, cappe...  30.4 us
    psum x1, waiting for transfers between devices, normalize_rows(): ffn = lax.psum(ffn, 'mp')  20.6 us
    mul x1, other arithmetic, dequant_down(): grouped = codes.reshape(scales.shape[0], -1, cols) * scales[:, None, :]  17.8 us
    all_gather x1, waiting for transfers between devices, on_device(): lax.all_gather(hidden, 'fsdp', axis=0, tiled=True)  16.6 us
    dot_general x1, matrix products, on_device(): jnp.dot(lax.all_gather(hidden, 'fsdp', axis=0, tiled=True), local_weight,...  15.8 us
    unnamed x1, blocking collectives  15.3 us
    psum x1, blocking collectives, on_device(): lax.psum((jnp.sum(token_loss), jnp.sum(weights)), ('fsdp', 'sub'))  14.2 us
    all_to_all x1, blocking collectives, on_device(): lax.all_to_all(partial_cols, 'fsdp', split_axis=0, concat_axis=1, tiled=T...  9.71 us
  transfers between devices with their start and end apart: 3, of which 2 were waited for; matrix products, arithmetic and copies ran while one was open for 13% of the time, Pallas kernels for 0%

profile of v1, /device:TPU:0, one launch (start us, length us, event | category | flops | bytes accessed | tf_op | source)
XLA Modules:
  0.0 177.6 jit_solution(14367403783102617484)
XLA Ops:
  7.2 0.7 all-gather.2.cloned.1.call-update
  7.9 0.0 all-reduce.5.cloned.1.call-start
  8.0 0.1 shift_left.56
  8.1 17.8 %fusion.2 = bf16[18432,1152]{1,0:T(8,128)(2,1)} fusion(s32[18432]{0:T(1024)S(1)} %broadcast_bitcast_fusion, s32[2304,1152]{1,0:T(8,128)} %param.12, bf16[144,1152]{1,0:T(8,128)(2,1)} %param.13), kind=kLoop, calls=%fused_computation.3 | loop fusion | flops 148635648 | bytes 53489664 | tf_op jit(solution)/shard_map/mul | solution.py:24
  26.0 16.6 %all-gather.2.cloned.1.call-done = bf16[32,18432]{1,0:T(8,128)(2,1)} async-done(((bf16[8,18432]{1,0:T(8,128)(2,1)}), bf16[32,18432]{1,0:T(8,128)(2,1)}) %all-gather.2.cloned.1.call-update) | async-done | bytes 1179664 | tf_op jit(solution)/shard_map/all_gather | solution.py:59
  42.6 15.8 %convolution_bitcast_fusion = f32[4,8,1152]{2,1,0:T(8,128)S(1)} fusion(bf16[32,18432]{1,0:T(8,128)(2,1)} %all-gather.2.cloned.1.call-done, bf16[18432,1152]{1,0:T(8,128)(2,1)} %fusion.2), kind=kOutput, calls=%fused_computation.6 | convolution fusion | flops 1358954496 | bytes 43794432 | tf_op jit(solution)/shard_map/dot_general | solution.py:58
  58.4 9.7 %all_to_all.24 = f32[4,8,1152]{2,1,0:T(8,128)} all-to-all(f32[4,8,1152]{2,1,0:T(8,128)S(1)} %convolution_bitcast_fusion), channel_id=1, replica_groups=mesh['groups'=2,'fsdp'=4,'mp'=2,'sub'=2] {'fsdp'}, dimensions={0} | all-to-all | bytes 294912 | tf_op jit(solution)/shard_map/all_to_all | solution.py:63
  68.1 20.6 %all-reduce.5.cloned.1.call-done = f32[8,4608]{1,0:T(8,128)} async-done(((f32[8,4608]{1,0:T(8,128)}), f32[8,4608]{1,0:T(8,128)}) %all-reduce.5.cloned.1.call-update) | async-done | bytes 147472 | tf_op jit(solution)/shard_map/psum | solution.py:36
  88.7 1.1 multiply_reduce_fusion.1
  89.8 1.1 multiply_reduce_fusion
  90.9 1.0 multiply_convert_fusion
  91.9 0.9 stack.2
  92.8 4.6 %all-to-all-start.1 = ((bf16[8,8,4608]{2,1,0:T(8,128)(2,1)}), bf16[8,8,4608]{2,1,0:T(8,128)(2,1)S(1)}, u32[]{:S(2)}, u32[]{:S(2)}) async-start(bf16[8,8,4608]{2,1,0:T(8,128)(2,1)} %stack.2), calls=%async_computation.1 | async-start | bytes 1179648 | tf_op jit(solution)/shard_map/all_to_all | solution.py:12
  97.4 0.1 shift_left.63
  97.5 0.1 shift_left.64
  97.6 0.6 dynamic-slice
  98.8 0.2 dynamic-update-slice
  99.1 15.3 %all-reduce = s32[64]{0:T(128)S(1)} all-reduce(s32[64]{0:T(128)S(1)} %dynamic-update-slice), channel_id=1, replica_groups=mesh['groups'=2,'fsdp'=4,'mp'=2,'sub'=2] {'fsdp','sub'}, use_global_device_ids=true, to_apply=%add | all-reduce | flops 64 | bytes 512
  114.3 1.2 shift_left.61
  115.6 3.5 %fusion.3 = bf16[512,36,128]{0,2,1:T(8,128)(2,1)} fusion(s32[512,36,128]{0,2,1:T(8,128)S(1)} %bitcast.31, s32[36,128]{1,0:T(8,128)S(1)} %shift_left.64, bf16[512,36]{0,1:T(8,128)(2,1)S(1)} %copy-done.3), kind=kLoop, calls=%fused_computation.5 | loop fusion | flops 16515072 | bytes 14211072 | tf_op jit(solution)/shard_map/mul | solution.py:31
  119.1 3.4 %exponential_reduce_fusion = (f32[64]{0:T(128)S(1)}, f32[64]{0:T(128)S(1)}) fusion(s32[512]{0:T(512)S(1)} %iota_add_fusion, s32[64]{0:T(128)S(1)} %all-reduce, bf16[512,4608]{0,1:T(8,128)(2,1)} %bitcast.32, bf16[8,8,4608]{2,1,0:T(8,128)(2,1)S(1)} %all-to-all-done.1), kind=kOutput, calls=%fused_computation.16 | convolution fusion | flops 302186368 | bytes 5311232 | tf_op jit(solution)/shard_map/dot_general | solution.py:70
  122.5 30.4 %all-reduce.1 = (f32[64]{0:T(128)S(1)}, f32[64]{0:T(128)S(1)}) all-reduce(f32[64]{0:T(128)S(1)} %get-tuple-element.3, f32[64]{0:T(128)S(1)} %get-tuple-element.2), channel_id=1, replica_groups=mesh['groups'=2,'fsdp'=4,'mp'=2,'sub'=2] {'fsdp','mp','sub'}, use_global_device_ids=true, to_apply=%region_6.7 | all-reduce | flops 128 | bytes 1024 | tf_op jit(solution)/shard_map/psum | solution.py:78
  152.9 1.3 fusion.7
  154.2 14.2 %all-reduce.2 = (f32[]{:T(128)}, f32[]{:T(128)}) all-reduce(f32[]{:T(128)} %get-tuple-element.8, f32[]{:T(128)} %get-tuple-element.10), channel_id=1, replica_groups=mesh['groups'=2,'fsdp'=4,'mp'=2,'sub'=2] {'fsdp','sub'}, use_global_device_ids=true, to_apply=%region_8.9 | all-reduce | flops 2 | bytes 16 | tf_op jit(solution)/shard_map/psum | solution.py:87
  (26 shorter events, 0.1 us)
Async XLA Ops:
  7.2 35.4 %all-gather.2.cloned.1.call-start = ((), (), s32[]{:S(2)}) async-start(), calls=%async_computation.2 | async-start | bytes 1474560 | tf_op jit(solution)/shard_map/all_gather | solution.py:59
  7.9 80.8 %all-reduce.5.cloned.1.call-start = ((), (), s32[]{:S(2)}) async-start(), calls=%async_computation.3 | async-start | bytes 294912 | tf_op jit(solution)/shard_map/psum | solution.py:36
  25.9 63.8 %copy-start.1 = (bf16[8,4608]{1,0:T(8,128)(2,1)S(1)}, bf16[8,4608]{1,0:T(8,128)(2,1)}, u32[]{:S(2)}) copy-start(bf16[8,4608]{1,0:T(8,128)(2,1)} %param.11) | copy-start | bytes 221188
  25.9 63.8 %copy-start.2 = (f32[4608]{0:T(1024)S(1)}, f32[4608]{0:T(1024)}, u32[]{:S(2)}) copy-start(f32[4608]{0:T(1024)} %param.14) | copy-start | bytes 55300
  25.9 65.0 %copy-start.4 = (f32[4608]{0:T(1024)S(1)}, f32[4608]{0:T(1024)}, u32[]{:S(2)}) copy-start(f32[4608]{0:T(1024)} %param.15) | copy-start | bytes 55300
  25.9 71.6 %copy-start.7 = (u32[32]{0:T(128)S(1)}, u32[32]{0:T(128)}, u32[]{:S(2)}) copy-start(u32[32]{0:T(128)} %constant.48) | copy-start | bytes 388
  26.0 72.8 %copy-start.6 = (s32[8]{0:T(128)S(1)}, s32[8]{0:T(128)}, u32[]{:S(2)}) copy-start(s32[8]{0:T(128)} %param.18) | copy-start | bytes 100
  26.0 88.4 %copy-start = (s32[512,576]{0,1:T(8,128)S(1)}, s32[512,576]{0,1:T(8,128)}, u32[]{:S(2)}) copy-start(s32[512,576]{0,1:T(8,128)} %param.16) | copy-start | bytes 3538948
  58.4 57.2 %copy-start.3 = (bf16[512,36]{0,1:T(8,128)(2,1)S(1)}, bf16[512,36]{0,1:T(8,128)(2,1)}, u32[]{:S(2)}) copy-start(bf16[512,36]{0,1:T(8,128)(2,1)} %param.17) | copy-start | bytes 110596
  92.8 26.3 %all-to-all-start.1 = ((bf16[8,8,4608]{2,1,0:T(8,128)(2,1)}), bf16[8,8,4608]{2,1,0:T(8,128)(2,1)S(1)}, u32[]{:S(2)}, u32[]{:S(2)}) async-start(bf16[8,8,4608]{2,1,0:T(8,128)(2,1)} %stack.2), calls=%async_computation.1 | async-start | bytes 1179648 | tf_op jit(solution)/shard_map/all_to_all | solution.py:12
  115.5 37.4 %copy-start.5 = (s32[8]{0:T(128)S(1)}, s32[8]{0:T(128)}, u32[]{:S(2)}) copy-start(s32[8]{0:T(128)} %param.19) | copy-start | bytes 100
Sparse Core Ops, SparseCore 0:
  9.5 32.9 all-gather.1
  68.2 20.3 all-reduce.4
